TPU v7x, 32 devices: a whole 2x2x4 slice. The times are simulated.
32 devices in a mesh: walker: 2 (over x), owner: 4 (over y, core), replica: 4 (over z).
Axes of the slice: x: 2, y: 2, z: 4, core: 2. Of those that a mesh axis runs over, the one named last changes fastest.
Arguments:
- layer_inputs: bfloat16 [4, 61440, 832], P(None, ('walker', 'owner', 'replica')), may hold values from -6 to 6
- layer_grads: bfloat16 [4, 61440, 256], P(None, ('walker', 'owner', 'replica')), may hold values from -6 to 6
- local_energy: float32 [1024], P(('walker', 'owner', 'replica')), may hold values from -3 to 1
Outputs:
- step: float32 [4, 832, 256], replicated
All inputs are finite; a program needn't handle non-finite values.
Results may differ from a plain program's by a relative error of at most 0.003.
Values sent between devices are 32-bit elements; how exact they have to be, the bound alone decides.
No kernel may reach another device: no remote copies, remote signals or barrier semaphores. Data moves between devices by JAX's collectives and lax.ppermute only.
A program may use at most 128 MiB of HBM per device.

v0:
```python
import jax
import jax.numpy as jnp
from jax import lax
from jax.sharding import PartitionSpec as P


def shards(layer_inputs, layer_grads, local_energy):
    walk_count = lax.axis_size("walker")
    owner_count = lax.axis_size("owner")
    replica_count = lax.axis_size("replica")
    devices = walk_count * owner_count * replica_count
    per_walker = local_energy.shape[0]
    walkers = per_walker * devices
    layers, rows, width_in = layer_inputs.shape
    width_out = layer_grads.shape[2]
    all_rows = rows * devices
    total = lax.psum(jnp.sum(local_energy), ("walker", "owner", "replica"))
    centered = local_energy - total / walkers
    weighted = (
        (
            layer_grads.astype(jnp.float32).reshape(
                layers, per_walker, rows // per_walker, width_out
            )
            * centered[None, :, None, None]
        )
        .astype(jnp.bfloat16)
        .reshape(layers, rows, width_out)
    )
    dims = (((1,), (1,)), ((0,), (0,)))
    input_sums = lax.dot_general(
        layer_inputs, layer_inputs, dims, preferred_element_type=jnp.float32
    )
    output_sums = lax.dot_general(
        layer_grads, layer_grads, dims, preferred_element_type=jnp.float32
    )
    grad_sums = lax.dot_general(layer_inputs, weighted, dims, preferred_element_type=jnp.float32)
    sliced = (
        lax.psum_scatter(input_sums, "owner", scatter_dimension=0, tiled=True),
        lax.psum_scatter(output_sums, "owner", scatter_dimension=0, tiled=True),
        lax.psum_scatter(grad_sums, "owner", scatter_dimension=0, tiled=True),
    )
    own_input, own_output, own_grad = lax.psum(
        (sliced[0][0], sliced[1][0], sliced[2][0]), ("walker", "replica")
    )
    ain = own_input / all_rows + 0.1 * jnp.eye(width_in, dtype=jnp.float32)
    gout = own_output / all_rows + 0.1 * jnp.eye(width_out, dtype=jnp.float32)
    grad = own_grad * (2.0 / walkers)
    chol_in = jnp.linalg.cholesky(ain)
    chol_out = jnp.linalg.cholesky(gout)
    left = jax.scipy.linalg.cho_solve((chol_in, True), grad)
    precond = jax.scipy.linalg.cho_solve((chol_out, True), left.T).T
    partial_align = jnp.sum(precond * grad).reshape(1)
    gathered, aligns = (
        lax.all_gather(precond[None], "owner", axis=0, tiled=True),
        lax.all_gather(partial_align, "owner", axis=0, tiled=True),
    )
    return gathered * jnp.sqrt(layers * width_in * width_out / jnp.sum(aligns))


def solution(mesh):
    in_specs = (
        P(None, ("walker", "owner", "replica"), None),
        P(None, ("walker", "owner", "replica"), None),
        P(("walker", "owner", "replica")),
    )
    out_specs = P()
    return jax.shard_map(shards, mesh=mesh, in_specs=in_specs, out_specs=out_specs, check_vma=False)
```

profile of v0, /device:TPU:0, one launch (start us, length us, event | category | flops | bytes accessed | tf_op | source)
XLA Modules:
  0.0 751.3 jit_solution(12996751452500109084)
XLA Ops:
  6.5 5.8 fusion.103
  13.1 42.2 %psum.30 = f32[]{:T(128)} all-reduce(f32[]{:T(128)} %reduce_sum.27), channel_id=1, replica_groups=mesh['walker'=2,'owner'=4,'replica'=4] {'walker','owner','replica'}, use_global_device_ids=true, to_apply=%region_23.24 | all-reduce | flops 1 | bytes 8 | tf_op jit(solution)/shard_map/psum | solution.py:17
  56.1 11.3 %fusion.3 = f32[4,832,256]{2,1,0:T(8,128)} fusion(bf16[4,1920,832]{1,2,0:T(8,128)(2,1)} %param.3, bf16[4,1920,256]{2,1,0:T(8,128)(2,1)} %param.4, f32[1920]{0:T(1024)S(1)} %mul.45), kind=kOutput, calls=%fused_computation.13 | convolution fusion | flops 3277455360 | bytes 20127232 | tf_op jit(solution)/shard_map/dot_general | solution.py:36
  67.4 25.0 %fusion.104 = f32[4,832,832]{2,1,0:T(8,128)} fusion(bf16[4,1920,832]{1,2,0:T(8,128)(2,1)} %param.3), kind=kOutput, calls=%fused_computation.232 | convolution fusion | flops 10632560640 | bytes 23855104 | tf_op jit(solution)/shard_map/dot_general | solution.py:30
  92.5 14.5 %reduce-scatter.8.cloned.1.call-done = f32[1,832,256]{2,1,0:T(8,128)} async-done(((f32[4,832,256]{2,1,0:T(8,128)}), f32[1,832,256]{2,1,0:T(8,128)}) %reduce-scatter.8.cloned.1.call-update) | async-done | bytes 851984 | tf_op jit(solution)/shard_map/reduce_scatter | solution.py:40
  107.0 97.9 %reduce-scatter.6.cloned.1.call-done = f32[1,832,832]{2,1,0:T(8,128)} async-done(((f32[4,832,832]{2,1,0:T(8,128)}), f32[1,832,832]{2,1,0:T(8,128)}) %reduce-scatter.6.cloned.1.call-update) | async-done | bytes 2768912 | tf_op jit(solution)/shard_map/reduce_scatter | solution.py:38
  205.7 157.1 %all-reduce.8.cloned.1.call-done = (f32[832,256]{1,0:T(8,128)}, f32[832,832]{1,0:T(8,128)}, f32[256,256]{0,1:T(8,128)}) async-done(((f32[832,256]{1,0:T(8,128)}, f32[832,832]{1,0:T(8,128)}, f32[256,256]{0,1:T(8,128)}), (f32[832,256]{1,0:T(8,128)}, f32[832,832]{1,0:T(8,128)}, f32[256,256]{0,1:T(8,128)})) %all-reduce.8.cloned.1.call-update) | async-done | bytes 3883024 | tf_op jit(solution)/shard_map/psum | solution.py:42
  362.8 3.7 select_add_fusion
  366.5 4.5 copy.11
  371.0 2.3 fusion.2
  373.3 1.6 copy-done.3
  374.9 11.7 %cholesky.273 = f32[128,128]{1,0:T(8,128)S(1)} custom-call(f32[128,128]{1,0:T(8,128)S(1)} %cholesky.614), custom_call_target="Cholesky" | custom-call | tf_op jit(solution)/shard_map/jit(cholesky)/cholesky | solution.py:48
  390.1 11.7 %cholesky.237 = f32[128,128]{1,0:T(8,128)S(1)} custom-call(f32[128,128]{1,0:T(8,128)S(1)} %cholesky.611), custom_call_target="Cholesky" | custom-call | tf_op jit(solution)/shard_map/jit(cholesky)/cholesky | solution.py:49
  401.8 9.8 %custom-call.76 = f32[1,128,128]{1,2,0:T(8,128)S(1)} custom-call(f32[1,128,128]{2,1,0:T(8,128)S(1)} %get-tuple-element.59), custom_call_target="InvertDiagBlocksLowerTriangular" | custom-call | tf_op jit(solution)/shard_map/jit(cholesky)/cholesky | solution.py:49
  413.8 11.9 %cholesky.256 = f32[128,128]{1,0:T(8,128)S(1)} custom-call(f32[128,128]{1,0:T(8,128)S(1)} %convolution_subtract_fusion.19), custom_call_target="Cholesky" | custom-call | tf_op jit(solution)/shard_map/jit(cholesky)/cholesky | solution.py:49
  427.3 10.7 %custom-call.78 = f32[1,128,128]{1,2,0:T(8,128)S(1)} custom-call(f32[1,128,128]{2,1,0:T(8,128)} %get-tuple-element.76), custom_call_target="InvertDiagBlocksLowerTriangular" | custom-call | tf_op jit(solution)/shard_map/jit(cholesky)/cholesky | solution.py:48
  437.9 1.4 constant_dynamic-update-slice_fusion.29
  439.3 1.4 convolution_subtract_fusion.2
  441.4 12.5 %cholesky.496 = f32[128,128]{1,0:T(8,128)S(1)} custom-call(f32[128,128]{1,0:T(8,128)} %cholesky.618), custom_call_target="Cholesky" | custom-call | tf_op jit(solution)/shard_map/jit(cholesky)/cholesky | solution.py:48
  454.6 10.6 %custom-call.79 = f32[1,128,128]{1,2,0:T(8,128)S(1)} custom-call(f32[1,128,128]{2,1,0:T(8,128)} %get-tuple-element.73), custom_call_target="InvertDiagBlocksLowerTriangular" | custom-call | tf_op jit(solution)/shard_map/jit(cholesky)/cholesky | solution.py:48
  466.1 1.6 convolution_subtract_fusion.3
  467.7 11.7 %cholesky.517 = f32[128,128]{1,0:T(8,128)S(1)} custom-call(f32[128,128]{1,0:T(8,128)S(1)} %cholesky.623), custom_call_target="Cholesky" | custom-call | tf_op jit(solution)/shard_map/jit(cholesky)/cholesky | solution.py:48
  480.1 9.8 %custom-call.80 = f32[1,128,128]{1,2,0:T(8,128)S(1)} custom-call(f32[1,128,128]{2,1,0:T(8,128)S(1)} %get-tuple-element.70), custom_call_target="InvertDiagBlocksLowerTriangular" | custom-call | tf_op jit(solution)/shard_map/jit(cholesky)/cholesky | solution.py:48
  490.2 1.7 convolution_subtract_fusion.4
  491.9 11.7 %cholesky.536 = f32[128,128]{1,0:T(8,128)S(1)} custom-call(f32[128,128]{1,0:T(8,128)S(1)} %cholesky.628), custom_call_target="Cholesky" | custom-call | tf_op jit(solution)/shard_map/jit(cholesky)/cholesky | solution.py:48
  504.3 9.9 %custom-call.81 = f32[1,128,128]{1,2,0:T(8,128)S(1)} custom-call(f32[1,128,128]{2,1,0:T(8,128)S(1)} %get-tuple-element.67), custom_call_target="InvertDiagBlocksLowerTriangular" | custom-call | tf_op jit(solution)/shard_map/jit(cholesky)/cholesky | solution.py:48
  514.5 1.6 convolution_subtract_fusion.5
  516.2 11.7 %cholesky.555 = f32[128,128]{1,0:T(8,128)S(1)} custom-call(f32[128,128]{1,0:T(8,128)S(1)} %cholesky.633), custom_call_target="Cholesky" | custom-call | tf_op jit(solution)/shard_map/jit(cholesky)/cholesky | solution.py:48
  528.6 9.8 %custom-call.82 = f32[1,128,128]{1,2,0:T(8,128)S(1)} custom-call(f32[1,128,128]{2,1,0:T(8,128)S(1)} %get-tuple-element.64), custom_call_target="InvertDiagBlocksLowerTriangular" | custom-call | tf_op jit(solution)/shard_map/jit(cholesky)/cholesky | solution.py:48
  538.6 1.5 convolution_subtract_fusion.17
  540.1 11.9 %cholesky.575 = f32[128,128]{1,0:T(8,128)S(1)} custom-call(f32[128,128]{1,0:T(8,128)S(1)} %cholesky.638), custom_call_target="Cholesky" | custom-call | tf_op jit(solution)/shard_map/jit(cholesky)/cholesky | solution.py:48
  552.7 9.8 %custom-call.83 = f32[1,128,128]{1,2,0:T(8,128)S(1)} custom-call(f32[1,128,128]{2,1,0:T(8,128)S(1)} %get-tuple-element.61), custom_call_target="InvertDiagBlocksLowerTriangular" | custom-call | tf_op jit(solution)/shard_map/jit(cholesky)/cholesky | solution.py:48
  563.8 5.8 cholesky.596
  575.7 1.6 copy-done.1
  577.3 17.0 %while.3 = (s32[]{:T(128)}, f32[832,832]{1,0:T(8,128)}, s32[6,2]{0,1:T(2,128)S(1)}, f32[6,128,128]{2,1,0:T(8,128)S(1)}, s32[]{:T(128)}) while((s32[]{:T(128)}, f32[832,832]{1,0:T(8,128)}, s32[6,2]{0,1:T(2,128)S(1)}, f32[6,128,128]{2,1,0:T(8,128)S(1)}, s32[]{:T(128)}) %tuple.81), condition=%wide.while_cond.1, body=%wide.while_body.1.sunk | while | flops 2 | bytes 131181 | solution.py:50
  577.9 2.2 bitcast_dynamic-update-slice_fusion.5
  580.7 2.2 bitcast_dynamic-update-slice_fusion.5
  583.5 2.2 bitcast_dynamic-update-slice_fusion.5
  586.4 2.2 bitcast_dynamic-update-slice_fusion.5
  589.2 2.2 bitcast_dynamic-update-slice_fusion.5
  592.0 2.2 bitcast_dynamic-update-slice_fusion.5
  595.2 70.0 %custom-call.84 = f32[7,128,128]{1,2,0:T(8,128)S(1)} custom-call(f32[7,128,128]{2,1,0:T(8,128)} %pad_maximum_fusion), custom_call_target="InvertDiagBlocksLowerTriangular" | custom-call | tf_op jit(solution)/shard_map/jit(_cho_solve)/triangular_solve | solution.py:50
  680.3 5.5 while.2
  680.9 1.4 dynamic-slice.15
  685.8 20.8 %custom-call.77 = f32[2,128,128]{1,2,0:T(8,128)S(1)} custom-call(f32[2,128,128]{2,1,0:T(8,128)} %get-tuple-element.12), custom_call_target="InvertDiagBlocksLowerTriangular" | custom-call | tf_op jit(solution)/shard_map/jit(_cho_solve)/triangular_solve | solution.py:51
  714.0 6.4 all-reduce.4
  721.6 18.8 %all-gather.3.cloned.1.call-done = f32[3328,256]{1,0:T(8,128)} async-done(((f32[832,256]{1,0:T(8,128)}), f32[3328,256]{1,0:T(8,128)}) %all-gather.3.cloned.1.call-update) | async-done | bytes 3407888 | tf_op jit(solution)/shard_map/all_gather | solution.py:54
  740.3 3.9 broadcast_multiply_fusion
  (164 shorter events, 47.5 us)
Async XLA Ops:
  6.5 5.9 copy-start.9
  6.5 86.0 %reduce-scatter.4.cloned.1.call-start = ((), (), s32[]{:S(2)}) async-start(), calls=%async_computation.3 | async-start | bytes 1310720 | tf_op jit(solution)/shard_map/reduce_scatter | solution.py:39
  12.4 94.6 %reduce-scatter.8.cloned.1.call-start = ((), (), s32[]{:S(2)}) async-start(), calls=%async_computation.5 | async-start | bytes 4259840 | tf_op jit(solution)/shard_map/reduce_scatter | solution.py:40
  67.3 137.6 %reduce-scatter.6.cloned.1.call-start = ((), (), s32[]{:S(2)}) async-start(), calls=%async_computation.4 | async-start | bytes 14909440 | tf_op jit(solution)/shard_map/reduce_scatter | solution.py:38
  92.5 270.3 %all-reduce.8.cloned.1.call-start = ((), (), s32[]{:S(2)}) async-start(), calls=%async_computation.7 | async-start | bytes 8192000 | tf_op jit(solution)/shard_map/psum | solution.py:42
  205.0 535.3 %all-gather.3.cloned.1.call-start = ((), (), s32[]{:S(2)}) async-start(), calls=%async_computation.6 | async-start | bytes 4259840 | tf_op jit(solution)/shard_map/all_gather | solution.py:54
  366.5 4.5 copy-start
  373.3 1.6 copy-start.3
  374.9 12.6 %copy-start.5 = (f32[256,256]{0,1:T(8,128)S(1)}, f32[256,256]{0,1:T(8,128)}, u32[]{:S(2)}) copy-start(f32[256,256]{0,1:T(8,128)} %get-tuple-element.43) | copy-start | bytes 786436
  389.4 0.7 copy-start.6
  575.4 1.9 copy-start.7
  575.4 18.8 %copy-start.8 = (f32[128,64]{1,0:T(8,128)S(1)}, f32[128,64]{1,0:T(8,128)}, u32[]{:S(2)}) copy-start(f32[128,64]{1,0:T(8,128)} %pad_convert_fusion) | copy-start | bytes 98308
  575.7 1.6 copy-start.1
  594.2 72.4 %copy-start.2 = (f32[832,832]{1,0:T(8,128)S(1)}, f32[832,832]{1,0:T(8,128)}, u32[]{:S(2)}) copy-start(f32[832,832]{1,0:T(8,128)} %get-tuple-element.198) | copy-start | bytes 8306692
  708.2 2.9 copy-start.10
  708.2 3.5 copy-start.4
Sparse Core Ops, SparseCore 0:
  12.5 27.5 reduce-scatter.3
  67.5 39.5 reduce-scatter.7
  109.7 95.2 reduce-scatter.5
  208.8 153.9 all-reduce.7
  711.2 29.0 all-gather.2
where the time goes:
time: 760 us; the launch traced here: 751 us
  waiting for transfers between devices  288 us (38%)
  other arithmetic  285 us (38%)
  matrix products  69.5 us (9%)
  blocking collectives  48.5 us (6%)
  local copies, waits for them, and re-layouts  38.2 us (5%)
  between operations  21.5 us (3%)
    psum x1, waiting for transfers between devices, shards(): lax.psum((sliced[0][0], sliced[1][0], sliced[2][0]), ('walker', 'replica'))  157 us
    another operation x26, other arithmetic, shards(): chol_in = jnp.linalg.cholesky(ain)  143 us
    reduce_scatter x1, waiting for transfers between devices, shards(): lax.psum_scatter(input_sums, 'owner', scatter_dimension=0, tiled=True)  97.9 us
    another operation x7, other arithmetic, shards(): left = jax.scipy.linalg.cho_solve((chol_in, True), grad)  71.7 us
    psum x1, blocking collectives, shards(): total = lax.psum(jnp.sum(local_energy), ('walker', 'owner', 'replica'))  42.2 us
    another operation x6, other arithmetic, shards(): chol_out = jnp.linalg.cholesky(gout)  34.2 us
    dot_general x1, matrix products, shards(): lax.dot_general(layer_inputs, layer_inputs, dims, preferred_element_type=...  25 us
    another operation x28, local copies, waits for them, and re-layouts  22.3 us
  transfers between devices with their start and end apart: 5, of which 4 were waited for; matrix products, arithmetic and copies ran while one was open for 5% of the time, Pallas kernels for 0%

commit v1 on v0

--- a/solution.py
+++ b/solution.py
@@ -2,6 +2,11 @@
 import jax.numpy as jnp
 from jax import lax
 from jax.sharding import PartitionSpec as P
+
+
+def axis_by_axis(value, inner_axis, outer_axis):
+    partial = lax.psum(value, inner_axis)
+    return lax.psum(partial, outer_axis)
 
 
 def shards(layer_inputs, layer_grads, local_energy):
@@ -39,8 +44,8 @@
         lax.psum_scatter(output_sums, "owner", scatter_dimension=0, tiled=True),
         lax.psum_scatter(grad_sums, "owner", scatter_dimension=0, tiled=True),
     )
-    own_input, own_output, own_grad = lax.psum(
-        (sliced[0][0], sliced[1][0], sliced[2][0]), ("walker", "replica")
+    own_input, own_output, own_grad = axis_by_axis(
+        (sliced[0][0], sliced[1][0], sliced[2][0]), "replica", "walker"
     )
     ain = own_input / all_rows + 0.1 * jnp.eye(width_in, dtype=jnp.float32)
     gout = own_output / all_rows + 0.1 * jnp.eye(width_out, dtype=jnp.float32)

time: 760 us -> 870 us (1.14)
  waiting for transfers between devices: 288 us -> 393 us
    psum x1 -> x2, waiting for transfers between devices: 157 us -> 261 us  [the longest x1 154 us: axis_by_axis(): partial = lax.psum(value, inner_axis)]
  transfers between devices with their start and end apart: 5 -> 6, of which waited for: 4 -> 5; matrix products, arithmetic and copies ran while one was open for 5% -> 5% of each run, Pallas kernels for 0% -> 0%
where the time goes in v1:
time: 870 us; the launch traced here: 862 us
  waiting for transfers between devices  393 us (45%)
  other arithmetic  284 us (33%)
  matrix products  71.9 us (8%)
  blocking collectives  48.5 us (6%)
  local copies, waits for them, and re-layouts  41.9 us (5%)
  between operations  21.9 us (3%)
    psum x1, waiting for transfers between devices, axis_by_axis(): partial = lax.psum(value, inner_axis)  154 us
    another operation x26, other arithmetic, shards(): chol_in = jnp.linalg.cholesky(ain)  140 us
    psum x1, waiting for transfers between devices, axis_by_axis(): return lax.psum(partial, outer_axis)  106 us
    reduce_scatter x1, waiting for transfers between devices, shards(): lax.psum_scatter(input_sums, 'owner', scatter_dimension=0, tiled=True)  97.9 us
    another operation x7, other arithmetic, shards(): left = jax.scipy.linalg.cho_solve((chol_in, True), grad)  73.3 us
    psum x1, blocking collectives, shards(): total = lax.psum(jnp.sum(local_energy), ('walker', 'owner', 'replica'))  42.2 us
    another operation x6, other arithmetic, shards(): chol_out = jnp.linalg.cholesky(gout)  34 us
    another operation x28, local copies, waits for them, and re-layouts  26.9 us
  transfers between devices with their start and end apart: 6, of which 5 were waited for; matrix products, arithmetic and copies ran while one was open for 5% of the time, Pallas kernels for 0%

profile of v1, /device:TPU:0, one launch (start us, length us, event | category | flops | bytes accessed | tf_op | source)
XLA Modules:
  0.0 861.6 jit_solution(14161724656921550291)
XLA Ops:
  6.5 5.8 fusion.103
  13.1 42.2 %psum.53 = f32[]{:T(128)} all-reduce(f32[]{:T(128)} %reduce_sum.27), channel_id=1, replica_groups=mesh['walker'=2,'owner'=4,'replica'=4] {'walker','owner','replica'}, use_global_device_ids=true, to_apply=%region_25.26 | all-reduce | flops 1 | bytes 8 | tf_op jit(solution)/shard_map/psum | solution.py:22
  56.1 11.3 %fusion.3 = f32[4,832,256]{2,1,0:T(8,128)} fusion(bf16[4,1920,832]{1,2,0:T(8,128)(2,1)} %param.3, bf16[4,1920,256]{2,1,0:T(8,128)(2,1)} %param.4, f32[1920]{0:T(1024)S(1)} %mul.45), kind=kOutput, calls=%fused_computation.13 | convolution fusion | flops 3277455360 | bytes 20127232 | tf_op jit(solution)/shard_map/dot_general | solution.py:41
  67.4 25.0 %fusion.104 = f32[4,832,832]{2,1,0:T(8,128)} fusion(bf16[4,1920,832]{1,2,0:T(8,128)(2,1)} %param.3), kind=kOutput, calls=%fused_computation.232 | convolution fusion | flops 10632560640 | bytes 23855104 | tf_op jit(solution)/shard_map/dot_general | solution.py:35
  92.5 14.5 %reduce-scatter.8.cloned.1.call-done = f32[1,832,256]{2,1,0:T(8,128)} async-done(((f32[4,832,256]{2,1,0:T(8,128)}), f32[1,832,256]{2,1,0:T(8,128)}) %reduce-scatter.8.cloned.1.call-update) | async-done | bytes 851984 | tf_op jit(solution)/shard_map/reduce_scatter | solution.py:45
  107.0 97.9 %reduce-scatter.6.cloned.1.call-done = f32[1,832,832]{2,1,0:T(8,128)} async-done(((f32[4,832,832]{2,1,0:T(8,128)}), f32[1,832,832]{2,1,0:T(8,128)}) %reduce-scatter.6.cloned.1.call-update) | async-done | bytes 2768912 | tf_op jit(solution)/shard_map/reduce_scatter | solution.py:43
  205.0 154.2 %all-reduce.10.cloned.1.call-done = (f32[832,256]{1,0:T(8,128)}, f32[832,832]{1,0:T(8,128)}, f32[256,256]{0,1:T(8,128)}) async-done(((f32[832,256]{1,0:T(8,128)}, f32[832,832]{1,0:T(8,128)}, f32[256,256]{0,1:T(8,128)}), (f32[832,256]{1,0:T(8,128)}, f32[832,832]{1,0:T(8,128)}, f32[256,256]{0,1:T(8,128)})) %all-reduce.10.cloned.1.call-update) | async-done | bytes 3883024 | tf_op jit(solution)/shard_map/psum | solution.py:8
  360.2 106.4 %all-reduce.12.cloned.1.call-done = (f32[832,256]{1,0:T(8,128)}, f32[832,832]{1,0:T(8,128)}, f32[256,256]{0,1:T(8,128)}) async-done(((f32[832,256]{1,0:T(8,128)}, f32[832,832]{1,0:T(8,128)}, f32[256,256]{0,1:T(8,128)}), (f32[832,256]{1,0:T(8,128)}, f32[832,832]{1,0:T(8,128)}, f32[256,256]{0,1:T(8,128)})) %all-reduce.12.cloned.1.call-update) | async-done | bytes 3883024 | tf_op jit(solution)/shard_map/psum | solution.py:9
  468.9 11.7 %cholesky.237 = f32[128,128]{1,0:T(8,128)S(1)} custom-call(f32[128,128]{1,0:T(8,128)S(1)} %cholesky.611), custom_call_target="Cholesky" | custom-call | tf_op jit(solution)/shard_map/jit(cholesky)/cholesky | solution.py:54
  480.6 9.8 %custom-call.76 = f32[1,128,128]{1,2,0:T(8,128)S(1)} custom-call(f32[1,128,128]{2,1,0:T(8,128)S(1)} %get-tuple-element.62), custom_call_target="InvertDiagBlocksLowerTriangular" | custom-call | tf_op jit(solution)/shard_map/jit(cholesky)/cholesky | solution.py:54
  490.9 11.7 %cholesky.256 = f32[128,128]{1,0:T(8,128)S(1)} custom-call(f32[128,128]{1,0:T(8,128)S(1)} %convolution_subtract_fusion.19), custom_call_target="Cholesky" | custom-call | tf_op jit(solution)/shard_map/jit(cholesky)/cholesky | solution.py:54
  503.0 1.9 select_add_fusion
  504.9 4.6 copy.11
  509.5 2.3 fusion.2
  511.8 1.6 copy-done.3
  513.4 11.7 %cholesky.273 = f32[128,128]{1,0:T(8,128)S(1)} custom-call(f32[128,128]{1,0:T(8,128)S(1)} %cholesky.614), custom_call_target="Cholesky" | custom-call | tf_op jit(solution)/shard_map/jit(cholesky)/cholesky | solution.py:53
  530.5 5.7 while.2
  531.1 1.4 dynamic-slice.15
  536.2 21.2 %custom-call.77 = f32[2,128,128]{1,2,0:T(8,128)} custom-call(f32[2,128,128]{2,1,0:T(8,128)} %get-tuple-element.12), custom_call_target="InvertDiagBlocksLowerTriangular" | custom-call | tf_op jit(solution)/shard_map/jit(_cho_solve)/triangular_solve | solution.py:56
  557.4 9.8 %custom-call.78 = f32[1,128,128]{1,2,0:T(8,128)S(1)} custom-call(f32[1,128,128]{2,1,0:T(8,128)S(1)} %get-tuple-element.79), custom_call_target="InvertDiagBlocksLowerTriangular" | custom-call | tf_op jit(solution)/shard_map/jit(cholesky)/cholesky | solution.py:53
  570.8 11.7 %cholesky.496 = f32[128,128]{1,0:T(8,128)S(1)} custom-call(f32[128,128]{1,0:T(8,128)S(1)} %cholesky.618), custom_call_target="Cholesky" | custom-call | tf_op jit(solution)/shard_map/jit(cholesky)/cholesky | solution.py:53
  582.6 9.8 %custom-call.79 = f32[1,128,128]{1,2,0:T(8,128)S(1)} custom-call(f32[1,128,128]{2,1,0:T(8,128)S(1)} %get-tuple-element.76), custom_call_target="InvertDiagBlocksLowerTriangular" | custom-call | tf_op jit(solution)/shard_map/jit(cholesky)/cholesky | solution.py:53
  593.8 1.6 convolution_subtract_fusion.3
  596.1 12.1 %cholesky.517 = f32[128,128]{1,0:T(8,128)S(1)} custom-call(f32[128,128]{1,0:T(8,128)S(1)} %cholesky.623), custom_call_target="Cholesky" | custom-call | tf_op jit(solution)/shard_map/jit(cholesky)/cholesky | solution.py:53
  608.9 9.8 %custom-call.80 = f32[1,128,128]{1,2,0:T(8,128)S(1)} custom-call(f32[1,128,128]{2,1,0:T(8,128)S(1)} %get-tuple-element.73), custom_call_target="InvertDiagBlocksLowerTriangular" | custom-call | tf_op jit(solution)/shard_map/jit(cholesky)/cholesky | solution.py:53
  620.0 1.7 convolution_subtract_fusion.4
  622.3 11.7 %cholesky.536 = f32[128,128]{1,0:T(8,128)S(1)} custom-call(f32[128,128]{1,0:T(8,128)S(1)} %cholesky.628), custom_call_target="Cholesky" | custom-call | tf_op jit(solution)/shard_map/jit(cholesky)/cholesky | solution.py:53
  634.8 9.8 %custom-call.81 = f32[1,128,128]{1,2,0:T(8,128)S(1)} custom-call(f32[1,128,128]{2,1,0:T(8,128)S(1)} %get-tuple-element.70), custom_call_target="InvertDiagBlocksLowerTriangular" | custom-call | tf_op jit(solution)/shard_map/jit(cholesky)/cholesky | solution.py:53
  645.8 1.6 convolution_subtract_fusion.5
  647.5 11.9 %cholesky.555 = f32[128,128]{1,0:T(8,128)S(1)} custom-call(f32[128,128]{1,0:T(8,128)S(1)} %cholesky.633), custom_call_target="Cholesky" | custom-call | tf_op jit(solution)/shard_map/jit(cholesky)/cholesky | solution.py:53
  660.1 9.8 %custom-call.82 = f32[1,128,128]{1,2,0:T(8,128)S(1)} custom-call(f32[1,128,128]{2,1,0:T(8,128)S(1)} %get-tuple-element.67), custom_call_target="InvertDiagBlocksLowerTriangular" | custom-call | tf_op jit(solution)/shard_map/jit(cholesky)/cholesky | solution.py:53
  670.1 1.5 convolution_subtract_fusion.17
  671.6 11.7 %cholesky.575 = f32[128,128]{1,0:T(8,128)S(1)} custom-call(f32[128,128]{1,0:T(8,128)S(1)} %cholesky.638), custom_call_target="Cholesky" | custom-call | tf_op jit(solution)/shard_map/jit(cholesky)/cholesky | solution.py:53
  684.1 9.8 %custom-call.83 = f32[1,128,128]{1,2,0:T(8,128)S(1)} custom-call(f32[1,128,128]{2,1,0:T(8,128)S(1)} %get-tuple-element.64), custom_call_target="InvertDiagBlocksLowerTriangular" | custom-call | tf_op jit(solution)/shard_map/jit(cholesky)/cholesky | solution.py:53
  695.2 5.8 cholesky.596
  707.2 1.6 copy-done.1
  708.8 21.3 %while.3 = (s32[]{:T(128)}, f32[832,832]{1,0:T(8,128)}, s32[6,2]{0,1:T(2,128)S(1)}, f32[6,128,128]{2,1,0:T(8,128)}, s32[]{:T(128)}) while((s32[]{:T(128)}, f32[832,832]{1,0:T(8,128)}, s32[6,2]{0,1:T(2,128)S(1)}, f32[6,128,128]{2,1,0:T(8,128)}, s32[]{:T(128)}) %tuple.83), condition=%wide.while_cond.1, body=%wide.while_body.1.sunk | while | flops 2 | bytes 132705 | solution.py:55
  709.5 2.9 bitcast_dynamic-update-slice_fusion.5
  713.0 2.9 bitcast_dynamic-update-slice_fusion.5
  716.6 2.9 bitcast_dynamic-update-slice_fusion.5
  720.1 2.9 bitcast_dynamic-update-slice_fusion.5
  723.6 2.9 bitcast_dynamic-update-slice_fusion.5
  727.2 2.9 bitcast_dynamic-update-slice_fusion.5
  730.2 1.9 pad_maximum_fusion
  732.1 70.4 %custom-call.84 = f32[7,128,128]{1,2,0:T(8,128)} custom-call(f32[7,128,128]{2,1,0:T(8,128)} %pad_maximum_fusion), custom_call_target="InvertDiagBlocksLowerTriangular" | custom-call | tf_op jit(solution)/shard_map/jit(_cho_solve)/triangular_solve | solution.py:55
  823.0 6.4 all-reduce.4
  830.7 19.7 %all-gather.3.cloned.1.call-done = f32[3328,256]{1,0:T(8,128)} async-done(((f32[832,256]{1,0:T(8,128)}), f32[3328,256]{1,0:T(8,128)}) %all-gather.3.cloned.1.call-update) | async-done | bytes 3407888 | tf_op jit(solution)/shard_map/all_gather | solution.py:59
  850.4 3.9 broadcast_multiply_fusion
  (171 shorter events, 53.0 us)
Async XLA Ops:
  6.5 5.9 copy-start.11
  6.5 86.0 %reduce-scatter.4.cloned.1.call-start = ((), (), s32[]{:S(2)}) async-start(), calls=%async_computation.3 | async-start | bytes 1310720 | tf_op jit(solution)/shard_map/reduce_scatter | solution.py:44
  12.4 94.6 %reduce-scatter.8.cloned.1.call-start = ((), (), s32[]{:S(2)}) async-start(), calls=%async_computation.5 | async-start | bytes 4259840 | tf_op jit(solution)/shard_map/reduce_scatter | solution.py:45
  67.3 137.6 %reduce-scatter.6.cloned.1.call-start = ((), (), s32[]{:S(2)}) async-start(), calls=%async_computation.4 | async-start | bytes 14909440 | tf_op jit(solution)/shard_map/reduce_scatter | solution.py:43
  92.5 266.8 %all-reduce.10.cloned.1.call-start = ((), (), s32[]{:S(2)}) async-start(), calls=%async_computation.7 | async-start | bytes 8192000 | tf_op jit(solution)/shard_map/psum | solution.py:8
  205.0 261.6 %all-reduce.12.cloned.1.call-start = ((), (), s32[]{:S(2)}) async-start(), calls=%async_computation.8 | async-start | bytes 8192000 | tf_op jit(solution)/shard_map/psum | solution.py:9
  359.3 491.1 %all-gather.3.cloned.1.call-start = ((), (), s32[]{:S(2)}) async-start(), calls=%async_computation.6 | async-start | bytes 4259840 | tf_op jit(solution)/shard_map/all_gather | solution.py:59
  466.6 36.4 %copy-start = (f32[832,832]{1,0:T(8,128)S(1)}, f32[832,832]{1,0:T(8,128)}, u32[]{:S(2)}) copy-start(f32[832,832]{1,0:T(8,128)} %get-tuple-element.45) | copy-start | bytes 8306692
  511.7 1.6 copy-start.3
  570.1 0.7 copy-start.6
  595.4 0.7 copy-start.7
  621.6 0.7 copy-start.8
  707.0 23.1 %copy-start.10 = (f32[128,64]{1,0:T(8,128)S(1)}, f32[128,64]{1,0:T(8,128)}, u32[]{:S(2)}) copy-start(f32[128,64]{1,0:T(8,128)} %pad_convert_fusion) | copy-start | bytes 98308
  707.2 1.6 copy-start.1
  730.1 74.9 %copy-start.2 = (f32[832,832]{1,0:T(8,128)S(1)}, f32[832,832]{1,0:T(8,128)}, u32[]{:S(2)}) copy-start(f32[832,832]{1,0:T(8,128)} %get-tuple-element.207) | copy-start | bytes 8306692
  802.5 4.2 copy-start.5
  813.3 2.3 copy-start.9
  817.2 2.9 copy-start.12
  817.2 3.5 copy-start.4
Sparse Core Ops, SparseCore 0:
  12.5 27.5 reduce-scatter.3
  67.5 39.5 reduce-scatter.7
  109.7 95.2 reduce-scatter.5
  207.4 151.8 all-reduce.9
  361.7 104.8 all-reduce.11
  820.3 30.0 all-gather.2
